TPU v7x, 32 devices: a whole 2x2x4 slice. The times are simulated.
32 devices in a mesh: layer: 8 (over z, y), dp: 4 (over x, core).
Axes of the slice: x: 2, y: 2, z: 4, core: 2. Of those that a mesh axis runs over, the one named last changes fastest.
Arguments:
- states: bfloat16 [8, 1024, 512], P('layer', 'dp'), may hold values from -40 to 40
- guess: bfloat16 [8, 1024, 512], P('layer', 'dp'), may hold values from -6 to 6
- cotangent: bfloat16 [1024, 512], P('dp'), may hold values from -6 to 6
- lengths: int32 [4], P('dp'), may hold values from 128 to 256
- coarse_rate: float32 [8, 512], P('layer'), may hold values from 0.2 to 1
- w_qkv: bfloat16 [8, 512, 1536], P('layer'), may hold values from -0.25 to 0.25
- w_out: bfloat16 [8, 512, 512], P('layer'), may hold values from -0.25 to 0.25
- w_in: bfloat16 [8, 512, 2048], P('layer'), may hold values from -0.25 to 0.25
- w_back: bfloat16 [8, 2048, 512], P('layer'), may hold values from -0.125 to 0.125
- gain_attn: float32 [8, 512], P('layer'), may hold values from 0.5 to 1.5
- gain_ffn: float32 [8, 512], P('layer'), may hold values from 0.5 to 1.5
Outputs:
- adjoint: bfloat16 [8, 1024, 512], P('layer', 'dp')
- coarse_error: float32 [8, 1024, 512], P('layer', 'dp')
- grad_qkv: float32 [8, 512, 1536], P('layer', 'dp')
- grad_out: float32 [8, 512, 512], P('layer', 'dp')
- grad_in: float32 [8, 512, 2048], P('layer', 'dp')
- grad_back: float32 [8, 2048, 512], P('layer', 'dp')
- grad_gain_attn: float32 [8, 512], P('layer', 'dp')
- grad_gain_ffn: float32 [8, 512], P('layer', 'dp')
All inputs are finite; a program needn't handle non-finite values.
Results may differ from a plain program's by a relative error of at most 0.028.
The roundings to bfloat16 on the way count: a program that leaves them out, or rounds other values in their place, can miss the bound.
Values may be sent and summed in bfloat16 or wider, within the bound.
A program may use at most 128 MiB of HBM per device.

v0:
```python
import functools

import jax
import jax.numpy as jnp
from jax import lax
from jax.experimental import pallas as pl
from jax.experimental.pallas import tpu as pltpu
from jax.sharding import PartitionSpec as P

HEAD_DIM = 64
SEQ = 256
FACTOR = 4
EPS = 1e-05
DEPTH_GAIN = 6.73
CUBIC = 0.044715
TANH_SCALE = 0.7978845608028654
F32 = jnp.float32
BF = jnp.bfloat16


def nn(a, b):
    return lax.dot_general(a, b, (((1,), (0,)), ((), ())), preferred_element_type=F32)


def nt(a, b):
    return lax.dot_general(a, b, (((1,), (1,)), ((), ())), preferred_element_type=F32)


def tn(a, b):
    return lax.dot_general(a, b, (((0,), (0,)), ((), ())), preferred_element_type=F32)


def mean(v):
    return jnp.mean(v, axis=-1, keepdims=True)


def unit_of(v):
    center = v - mean(v)
    inv = lax.rsqrt(mean(center * center) + EPS)
    return center * inv, inv


def norm_back(up, unit, inv, gain):
    scaled = up * gain
    inner = scaled - mean(scaled) - unit * mean(scaled * unit)
    return inv * inner, jnp.sum(up * unit, axis=0, keepdims=True)


def kernel(
    layers, dpn, coarse,
    len_ref, x_ref, guess_ref, cot_ref, rate_ref, gain1_ref, gain2_ref,
    wqkv_hbm, wout_hbm, win_hbm, wback_hbm,
    adj_ref, err_out, gqkv_ref, gout_ref, gin_ref, gback_ref, g1_ref, g2_ref,
    wqkv, wout, win, wback,
    qkv, bias, probs, ctx, unit1, unit2, inv1, inv2, normed_bf, hidden, deriv,
    up_bf, dctx, dqkv, dpre, dfirst, relaxed,
    above, above2, crel, cguess, crate, err,
    part_back, part_in, part_out, part_qkv,
    r1_back, r1_in, r1_out, r1_qkv,
    r2_back, r2_in, r2_out, r2_qkv,
    gsum, grecv,
    wsem, s_up, r_up, s_cg, r_cg, s_cr, r_cr, s_ce, r_ce,
    s1, q1, s2, q2, s_g, r_g,
):
    layer = lax.axis_index("layer")
    dp = lax.axis_index("dp")
    tokens, width = x_ref.shape
    hidden_units = hidden.shape[1]
    sentences = tokens // SEQ
    pairs = width // 128
    scale = HEAD_DIM ** (-0.5)
    chips = dpn // 2
    chip, core = dp // 2, dp % 2
    last = layers - 1
    is_last = layer == last
    is_coarse = (layer % FACTOR == 0) | is_last
    next_coarse = (((layer + 1) % FACTOR == 0) | (layer + 1 == last)) & (layer < last)
    next_plain = (layer < last) & (((layer + 1) % FACTOR != 0) & (layer + 1 != last))

    def send(src, dst, ssem, rsem, **where):
        return pltpu.make_async_remote_copy(
            src_ref=src, dst_ref=dst, send_sem=ssem, recv_sem=rsem,
            device_id=where, device_id_type=pl.DeviceIdType.MESH,
        )

    loads = [
        pltpu.make_async_copy(a, b, wsem.at[i])
        for i, (a, b) in enumerate(
            ((wqkv_hbm, wqkv), (wout_hbm, wout), (win_hbm, win), (wback_hbm, wback))
        )
    ]
    for load in loads:
        load.start()

    barrier = pltpu.get_barrier_semaphore()
    for o in range(1, layers):
        pl.semaphore_signal(
            barrier, inc=1, device_id={"layer": lax.rem(layer + o, layers)},
            device_id_type=pl.DeviceIdType.MESH,
        )
    for o in range(1, dpn):
        pl.semaphore_signal(
            barrier, inc=1, device_id={"dp": lax.rem(dp + o, dpn)},
            device_id_type=pl.DeviceIdType.MESH,
        )
    pl.semaphore_wait(barrier, layers - 1 + dpn - 1)

    def targets(j):
        urgent = [t for t in range(j) if t + 1 in coarse and t not in coarse]
        rest = [t for t in range(j) if t not in urgent]
        return urgent[::-1] + rest[::-1]

    up_guess = lambda: send(
        guess_ref, above, s_up.at[0], r_up.at[0], layer=jnp.maximum(layer - 1, 0)
    )
    up_relaxed = lambda: send(
        relaxed, above2, s_up.at[1], r_up.at[1], layer=jnp.maximum(layer - 1, 0)
    )

    def coarse_sends(src, dst, ssem, rsem, act):
        for idx, j in enumerate(coarse):

            @pl.when(layer == j)
            def _():
                for n, t in enumerate(targets(j)):
                    act(send(src, dst.at[idx], ssem.at[n], rsem.at[idx], layer=jnp.int32(t)))

    pl.when(layer > 0)(lambda: up_guess().start())
    start = lambda c: c.start()
    coarse_sends(guess_ref, cguess, s_cg, r_cg, start)
    coarse_sends(rate_ref, crate, s_cr, r_cr, start)

    gain1, gain2 = gain1_ref[...], gain2_ref[...]
    loads[0].wait()
    qkv[...] = nn(x_ref[...], wqkv[...]).astype(BF)
    for s in range(sentences):
        rows = pl.ds(s * SEQ, SEQ)
        row_at = lax.broadcasted_iota(jnp.int32, (SEQ, SEQ), 0)
        col_at = lax.broadcasted_iota(jnp.int32, (SEQ, SEQ), 1)
        bias[...] = jnp.where((col_at <= row_at) & (col_at < len_ref[s]), 0.0, -1e30)

        def attend(i, carry):
            lanes = lambda k: pl.ds(pl.multiple_of(k * width + i * 128, 128), 128)
            q, k, v = qkv[rows, lanes(0)], qkv[rows, lanes(1)], qkv[rows, lanes(2)]
            outs = []
            for h in range(2):
                cut = slice(h * HEAD_DIM, (h + 1) * HEAD_DIM)
                sc = nt(q[:, cut], k[:, cut]) * scale + bias[...]
                e = jnp.exp(sc - jnp.max(sc, axis=-1, keepdims=True))
                p = e * (1.0 / jnp.sum(e, axis=-1, keepdims=True))
                probs[s, 2 * i + h] = p
                outs.append(nn(p.astype(BF), v[:, cut]))
            ctx[rows, lanes(0)] = jnp.concatenate(outs, axis=-1).astype(BF)
            return carry

        lax.fori_loop(0, pairs, attend, 0)
    loads[1].wait()
    u, iv = unit_of(DEPTH_GAIN * x_ref[...].astype(F32) + nn(ctx[...], wout[...]))
    unit1[...] = u
    inv1[...] = iv
    normed_bf[...] = (u * gain1).astype(BF)
    loads[2].wait()
    step = 512

    def feed(i, carry):
        lanes = pl.ds(pl.multiple_of(i * step, step), step)
        pre = nn(normed_bf[...], win[:, lanes])
        sq = pre * pre
        t = jnp.tanh(TANH_SCALE * (pre + CUBIC * sq * pre))
        hidden[:, lanes] = (0.5 * pre * (1.0 + t)).astype(BF)
        deriv[:, lanes] = 0.5 * (1.0 + t) + 0.5 * pre * (1.0 - t * t) * TANH_SCALE * (
            1.0 + 3.0 * CUBIC * sq
        )
        return carry

    lax.fori_loop(0, hidden_units // step, feed, 0)
    loads[3].wait()
    u, iv = unit_of(DEPTH_GAIN * (unit1[...] * gain1) + nn(hidden[...], wback[...]))
    unit2[...] = u
    inv2[...] = iv

    grads = (
        (part_back, r1_back, r2_back, gback_ref),
        (part_in, r1_in, r2_in, gin_ref),
        (part_out, r1_out, r2_out, gout_ref),
        (part_qkv, r1_qkv, r2_qkv, gqkv_ref),
    )

    def near(g, i):
        part, r1, _, _ = grads[g]
        size = r1.shape[1]
        at = pl.multiple_of((2 * i + 1 - core) * size, size)
        return send(
            part.at[pl.ds(at, size)], r1.at[i], s1.at[g, i], q1.at[g, i],
            dp=2 * chip + 1 - core,
        )

    def far(g, o):
        _, r1, r2, _ = grads[g]
        i = lax.rem(chip + o, chips)
        return send(
            r1.at[i], r2.at[o - 1], s2.at[g, o - 1], q2.at[g, o - 1], dp=2 * i + core
        )

    def mine(g, i):
        part, r1, _, _ = grads[g]
        size = r1.shape[1]
        return part[pl.ds(pl.multiple_of((2 * i + core) * size, size), size)].astype(F32)

    def to_partner(g):
        for i in range(chips):
            near(g, i).start()

    def to_chips(g):
        r1 = grads[g][1]
        for i in range(chips):
            near(g, i).wait_recv()
        for o in range(1, chips):
            i = lax.rem(chip + o, chips)
            r1[i] = (r1[i].astype(F32) + mine(g, i)).astype(BF)
            far(g, o).start()

    def finish(g):
        _, r1, r2, out = grads[g]
        total = r1[chip].astype(F32) + mine(g, chip)
        for o in range(1, chips):
            far(g, o).wait_recv()
            total = total + r2[o - 1].astype(F32)
        out[...] = total.astype(out.dtype)

    def transposed(left, right, out):
        cols = min(step, left.shape[1])

        def body(i, carry):
            at = pl.ds(pl.multiple_of(i * cols, cols), cols)
            out[at, :] = tn(left[:, at], right).astype(BF)
            return carry

        lax.fori_loop(0, left.shape[1] // cols, body, 0)

    def backward(final):
        up = up_bf[...].astype(F32)
        d2, grad_two = norm_back(up, unit2[...], inv2[...], gain2)
        d2_bf = d2.astype(BF)
        dfirst[...] = DEPTH_GAIN * d2
        up_bf[...] = d2_bf

        if final:
            gsum[1:2, :] = grad_two
            transposed(hidden, up_bf[...], part_back)
            to_partner(0)

        def body(i, carry):
            lanes = pl.ds(pl.multiple_of(i * step, step), step)
            dh = nt(up_bf[...], wback[lanes, :])
            dpre[:, lanes] = (dh * deriv[:, lanes]).astype(BF)
            return carry

        lax.fori_loop(0, hidden_units // step, body, 0)
        if final:
            to_chips(0)
            transposed(normed_bf, dpre[...], part_in)
            to_partner(1)
        dn = dfirst[...] + nt(dpre[...], win[...])
        d1, grad_one = norm_back(dn, unit1[...], inv1[...], gain1)
        dfirst[...] = DEPTH_GAIN * d1
        up_bf[...] = d1.astype(BF)
        if final:
            gsum[0:1, :] = grad_one
            to_chips(1)
            transposed(ctx, up_bf[...], part_out)
            to_partner(2)
        dctx[...] = nt(up_bf[...], wout[...]).astype(BF)
        for s in range(sentences):
            rows = pl.ds(s * SEQ, SEQ)

            def attend(i, carry):
                lanes = lambda k: pl.ds(pl.multiple_of(k * width + i * 128, 128), 128)
                q, k, v = qkv[rows, lanes(0)], qkv[rows, lanes(1)], qkv[rows, lanes(2)]
                dc = dctx[rows, lanes(0)]
                outs = ([], [], [])
                for h in range(2):
                    cut = slice(h * HEAD_DIM, (h + 1) * HEAD_DIM)
                    p = probs[s, 2 * i + h]
                    dp_ = nt(dc[:, cut], v[:, cut])
                    outs[2].append(tn(p.astype(BF), dc[:, cut]))
                    ds = p * (dp_ - jnp.sum(p * dp_, axis=-1, keepdims=True)) * scale
                    ds = ds.astype(BF)
                    outs[0].append(nn(ds, k[:, cut]))
                    outs[1].append(tn(ds, q[:, cut]))
                for n in range(3):
                    dqkv[rows, lanes(n)] = jnp.concatenate(outs[n], axis=-1).astype(BF)
                return carry

            lax.fori_loop(0, pairs, attend, 0)
        if final:
            to_chips(2)
            transposed(x_ref, dqkv[...], part_qkv)
            to_partner(3)
        return (dfirst[...] + nt(dqkv[...], wqkv[...])).astype(BF)

    @pl.when(is_last)
    def _():
        up_bf[...] = cot_ref[...]

    @pl.when(layer < last)
    def _():
        up_guess().wait_recv()
        up_bf[...] = above[...]

    relaxed[...] = backward(False)
    plain_sender = (layer > 0) & jnp.logical_not(is_coarse)
    pl.when(plain_sender)(lambda: up_relaxed().start())
    coarse_sends(relaxed, crel, s_ce, r_ce, start)

    def build_err():
        err[...] = jnp.zeros_like(err)
        for idx in reversed(range(len(coarse))):

            @pl.when(layer < coarse[idx])
            def _():
                here = jnp.int32(0)
                send(guess_ref, cguess.at[idx], s_cg.at[0], r_cg.at[idx], layer=here).wait_recv()
                send(rate_ref, crate.at[idx], s_cr.at[0], r_cr.at[idx], layer=here).wait_recv()
                send(relaxed, crel.at[idx], s_ce.at[0], r_ce.at[idx], layer=here).wait_recv()
                err[...] = crate[idx] * err[...] + (
                    crel[idx].astype(F32) - cguess[idx].astype(F32)
                )

    @pl.when(is_last)
    def _():
        up_bf[...] = cot_ref[...]

    @pl.when(next_plain)
    def _():
        up_relaxed().wait_recv()
        up_bf[...] = above2[...]

    @pl.when(next_coarse)
    def _():
        build_err()
        up_bf[...] = (above[...].astype(F32) + err[...]).astype(BF)

    adj_ref[...] = backward(True)

    def gain_send(o):
        return send(
            gsum, grecv.at[o - 1], s_g.at[o - 1], r_g.at[o - 1], dp=lax.rem(dp + o, dpn)
        )

    for o in range(1, dpn):
        gain_send(o).start()
    to_chips(3)
    pl.when(jnp.logical_not(next_coarse))(build_err)

    @pl.when(is_coarse)
    def _():
        own = guess_ref[...].astype(F32)
        err[...] = rate_ref[...] * err[...] + (relaxed[...].astype(F32) - own)
        adj_ref[...] = (own + err[...]).astype(BF)

    err_out[...] = err[...]
    finish(0)
    finish(1)
    gains = gsum[...]
    for o in range(1, dpn):
        gain_send(o).wait_recv()
        gains = gains + grecv[o - 1]
    piece = width // dpn
    one, two = jnp.zeros((1, piece), F32), jnp.zeros((1, piece), F32)
    for c in range(dpn):
        cut = slice(c * piece, (c + 1) * piece)
        here = dp == c
        one = one + jnp.where(here, gains[0:1, cut], 0.0)
        two = two + jnp.where(here, gains[1:2, cut], 0.0)
    g1_ref[...] = one
    g2_ref[...] = two
    finish(2)
    finish(3)

    sent = lambda c: c.wait_send()
    pl.when(layer > 0)(lambda: sent(up_guess()))
    pl.when(plain_sender)(lambda: sent(up_relaxed()))
    coarse_sends(guess_ref, cguess, s_cg, r_cg, sent)
    coarse_sends(rate_ref, crate, s_cr, r_cr, sent)
    coarse_sends(relaxed, crel, s_ce, r_ce, sent)
    for g in range(4):
        for i in range(chips):
            sent(near(g, i))
        for o in range(1, chips):
            sent(far(g, o))
    for o in range(1, dpn):
        sent(gain_send(o))


def on_device(layers, dpn, *args):
    (states, guess, cotangent, lengths, rate, w_qkv, w_out, w_in, w_back, gain1, gain2) = args
    tokens, width = states.shape[1:]
    ff = w_in.shape[2]
    heads = width // HEAD_DIM
    coarse = [j for j in range(1, layers) if j % FACTOR == 0 or j == layers - 1]
    n = len(coarse)
    chips = dpn // 2
    shapes = ((ff, width), (width, ff), (width, width), (width, 3 * width))
    vm = pltpu.VMEM
    rows = (tokens, width)
    dma = lambda *s: pltpu.SemaphoreType.DMA(s)
    scratch = [
        vm((width, 3 * width), BF), vm((width, width), BF), vm((width, ff), BF),
        vm((ff, width), BF),
        vm((tokens, 3 * width), BF), vm((SEQ, SEQ), F32),
        vm((tokens // SEQ, heads, SEQ, SEQ), F32), vm(rows, BF), vm(rows, F32), vm(rows, F32),
        vm((tokens, 1), F32), vm((tokens, 1), F32), vm(rows, BF), vm((tokens, ff), BF),
        vm((tokens, ff), F32),
        vm(rows, BF), vm(rows, BF), vm((tokens, 3 * width), BF), vm((tokens, ff), BF),
        vm(rows, F32), vm(rows, BF),
        vm(rows, BF), vm(rows, BF), vm((n,) + rows, BF), vm((n,) + rows, BF),
        vm((n, 1, width), F32), vm(rows, F32),
    ]
    scratch += [vm(s, BF) for s in shapes]
    scratch += [vm((chips, s[0] // dpn, s[1]), BF) for s in shapes]
    scratch += [vm((max(chips - 1, 1), s[0] // dpn, s[1]), BF) for s in shapes]
    scratch += [vm((2, width), F32), vm((dpn - 1, 2, width), F32)]
    far = max(chips - 1, 1)
    scratch += [
        dma(4), dma(2), dma(2), dma(layers), dma(n), dma(layers), dma(n), dma(layers), dma(n),
        dma(4, chips), dma(4, chips), dma(4, far), dma(4, far), dma(dpn - 1), dma(dpn - 1),
    ]
    whole = pl.BlockSpec(memory_space=pltpu.VMEM)
    left = pl.BlockSpec(memory_space=pl.ANY)
    out = lambda s, t: jax.ShapeDtypeStruct(s, t)
    piece = lambda s: out((s[0] // dpn, s[1]), BF)
    results = pl.pallas_call(
        functools.partial(kernel, layers, dpn, coarse),
        out_shape=(
            out(rows, BF), out(rows, F32), piece(shapes[3]), piece(shapes[2]), piece(shapes[1]),
            piece(shapes[0]), out((1, width // dpn), F32), out((1, width // dpn), F32),
        ),
        in_specs=[pl.BlockSpec(memory_space=pltpu.SMEM)] + [whole] * 6 + [left] * 4,
        out_specs=(whole,) * 8,
        scratch_shapes=scratch,
        compiler_params=pltpu.CompilerParams(
            collective_id=0, has_side_effects=True, vmem_limit_bytes=56 * 1024 * 1024
        ),
    )(
        lengths, states[0], guess[0], cotangent, rate, gain1, gain2,
        w_qkv[0], w_out[0], w_in[0], w_back[0],
    )
    adj, err, g_qkv, g_out, g_in, g_back, g_one, g_two = results
    return (
        adj[None], err[None], g_qkv.astype(F32)[None], g_out.astype(F32)[None],
        g_in.astype(F32)[None], g_back.astype(F32)[None], g_one, g_two,
    )


def solution(mesh):
    placed = (
        P("layer", "dp", None), P("layer", "dp", None), P("dp", None), P("dp"),
        P("layer", None), P("layer", None, None), P("layer", None, None),
        P("layer", None, None), P("layer", None, None), P("layer", None), P("layer", None),
    )
    split = P("layer", "dp", None)
    return jax.shard_map(
        functools.partial(on_device, mesh.shape["layer"], mesh.shape["dp"]),
        mesh=mesh,
        in_specs=placed,
        out_specs=(split,) * 6 + (P("layer", "dp"),) * 2,
        check_vma=False,
    )
```

profile of v0, /device:TPU:15, one launch (start us, length us, event | category | flops | bytes accessed | tf_op | source)
XLA Modules:
  0.0 97.9 jit_solution(7266660477581976438)
XLA Ops:
  1.3 88.0 %shard_map.170 = (bf16[256,512]{1,0:T(8,128)(2,1)}, f32[256,512]{1,0:T(8,128)}, bf16[128,1536]{1,0:T(8,128)(2,1)}, bf16[128,512]{1,0:T(8,128)(2,1)}, bf16[128,20...) custom-call(s32[1]{0:T(128)S(6)} %copy.23.len_ref, ...), custom_call_target="tpu_custom_call" | custom-call | tf_op jit(solution)/shard_map/pallas_call | solution.py:433
  89.3 0.0 copy-start.1
  89.3 0.0 copy-start.3
  89.3 0.0 copy-start.2
  89.3 2.2 %bitcast_convert_fusion = f32[1,512,512]{2,1,0:T(8,128)} fusion(bf16[512,512]{1,0:T(8,128)(2,1)} %get-tuple-element.21), kind=kLoop, calls=%fused_computation | loop fusion | flops 262144 | bytes 1572864 | tf_op jit(solution)/shard_map/broadcast_in_dim | solution.py:452
  91.5 0.0 copy-start
  91.5 0.0 copy-start.5
  91.5 0.0 copy-start.4
  91.5 2.2 %bitcast_convert_fusion.1 = f32[1,128,2048]{2,1,0:T(8,128)} fusion(bf16[128,2048]{1,0:T(8,128)(2,1)} %get-tuple-element.20), kind=kLoop, calls=%fused_computation.1 | loop fusion | flops 262144 | bytes 1572864 | tf_op jit(solution)/shard_map/broadcast_in_dim | solution.py:452
  93.7 0.0 copy-done.1
  93.7 1.0 bitcast_convert_fusion.2
  94.7 0.0 copy-done.3
  94.7 0.7 bitcast_convert_fusion.3
  95.4 0.0 copy-done.2
  95.4 0.7 copy.24
  96.1 0.0 copy-done
  96.1 0.8 copy.25
  96.9 0.0 copy-done.5
  96.9 0.5 copy.26
  97.4 0.0 copy-done.4
  97.4 0.5 copy.27
Async XLA Ops:
  89.3 4.4 %copy-start.1 = (bf16[128,1536]{1,0:T(8,128)(2,1)S(1)}, bf16[128,1536]{1,0:T(8,128)(2,1)}, u32[]{:S(2)}) copy-start(bf16[128,1536]{1,0:T(8,128)(2,1)} %get-tuple-element.18) | copy-start | bytes 1179652
  89.3 5.4 %copy-start.3 = (bf16[128,512]{1,0:T(8,128)(2,1)S(1)}, bf16[128,512]{1,0:T(8,128)(2,1)}, u32[]{:S(2)}) copy-start(bf16[128,512]{1,0:T(8,128)(2,1)} %get-tuple-element.19) | copy-start | bytes 393220
  89.3 6.1 %copy-start.2 = (bf16[256,512]{1,0:T(8,128)(2,1)S(1)}, bf16[256,512]{1,0:T(8,128)(2,1)}, u32[]{:S(2)}) copy-start(bf16[256,512]{1,0:T(8,128)(2,1)} %get-tuple-element.16) | copy-start | bytes 786436
  91.5 4.6 %copy-start = (f32[256,512]{1,0:T(8,128)S(1)}, f32[256,512]{1,0:T(8,128)}, u32[]{:S(2)}) copy-start(f32[256,512]{1,0:T(8,128)} %get-tuple-element.17) | copy-start | bytes 1572868
  91.5 5.4 %copy-start.5 = (f32[1,128]{1,0:T(1,128)S(1)}, f32[1,128]{1,0:T(1,128)}, u32[]{:S(2)}) copy-start(f32[1,128]{1,0:T(1,128)} %get-tuple-element.38) | copy-start | bytes 1540
  91.5 5.9 %copy-start.4 = (f32[1,128]{1,0:T(1,128)S(1)}, f32[1,128]{1,0:T(1,128)}, u32[]{:S(2)}) copy-start(f32[1,128]{1,0:T(1,128)} %get-tuple-element.39) | copy-start | bytes 1540
where the time goes:
time: 98.1 us; the launch traced here: 97.9 us
  Pallas kernels  88 us (90%)
  other arithmetic  6.08 us (6%)
  local copies, waits for them, and re-layouts  2.54 us (3%)
  between operations  1.32 us (1%)
    pallas_call x1, Pallas kernels, on_device(): pl.pallas_call(functools.partial(kernel, layers, dpn, coarse), out_shape=...  88 us
    unnamed x16, local copies, waits for them, and re-layouts  2.54 us
    broadcast_in_dim x1, other arithmetic, on_device(): g_back.astype(F32)[None]  2.21 us
    broadcast_in_dim x1, other arithmetic, on_device(): g_in.astype(F32)[None]  2.18 us

commit v1 on v0

--- a/solution.py
+++ b/solution.py
@@ -48,18 +48,19 @@
 
 def kernel(
     layers, dpn, coarse,
-    len_ref, x_ref, guess_ref, cot_ref, rate_ref, gain1_ref, gain2_ref,
+    len_ref, x_hbm, guess_hbm, cot_hbm, rate_hbm, gain1_hbm, gain2_hbm,
     wqkv_hbm, wout_hbm, win_hbm, wback_hbm,
-    adj_ref, err_out, gqkv_ref, gout_ref, gin_ref, gback_ref, g1_ref, g2_ref,
+    adj_ref, err_ref, gqkv_ref, gout_ref, gin_ref, gback_ref, g1_ref, g2_ref,
+    x_ref, guess_ref, cot_ref, rate_ref, gain1_ref, gain2_ref,
     wqkv, wout, win, wback,
     qkv, bias, probs, ctx, unit1, unit2, inv1, inv2, normed_bf, hidden, deriv,
     up_bf, dctx, dqkv, dpre, dfirst, relaxed,
-    above, above2, crel, cguess, crate, err,
+    above, above2, crel, cguess, crate, err, err_bf, err_in,
     part_back, part_in, part_out, part_qkv,
     r1_back, r1_in, r1_out, r1_qkv,
     r2_back, r2_in, r2_out, r2_qkv,
     gsum, grecv,
-    wsem, s_up, r_up, s_cg, r_cg, s_cr, r_cr, s_ce, r_ce,
+    wsem, lsem, s_up, r_up, s_cg, r_cg, s_cr, r_cr, s_ce, r_ce, s_lz, r_lz,
     s1, q1, s2, q2, s_g, r_g,
 ):
     layer = lax.axis_index("layer")
@@ -89,7 +90,17 @@
             ((wqkv_hbm, wqkv), (wout_hbm, wout), (win_hbm, win), (wback_hbm, wback))
         )
     ]
-    for load in loads:
+    small = [
+        pltpu.make_async_copy(a, b, lsem.at[i])
+        for i, (a, b) in enumerate(
+            (
+                (x_hbm, x_ref), (guess_hbm, guess_ref), (rate_hbm, rate_ref),
+                (gain1_hbm, gain1_ref), (gain2_hbm, gain2_ref),
+                (cot_hbm, cot_ref),
+            )
+        )
+    ]
+    for load in small[:3] + loads[:1] + small[3:] + loads[1:]:
         load.start()
 
     barrier = pltpu.get_barrier_semaphore()
@@ -105,10 +116,7 @@
         )
     pl.semaphore_wait(barrier, layers - 1 + dpn - 1)
 
-    def targets(j):
-        urgent = [t for t in range(j) if t + 1 in coarse and t not in coarse]
-        rest = [t for t in range(j) if t not in urgent]
-        return urgent[::-1] + rest[::-1]
+    tops = [(i, c - 1) for i, c in enumerate(coarse)]
 
     up_guess = lambda: send(
         guess_ref, above, s_up.at[0], r_up.at[0], layer=jnp.maximum(layer - 1, 0)
@@ -117,18 +125,33 @@
         relaxed, above2, s_up.at[1], r_up.at[1], layer=jnp.maximum(layer - 1, 0)
     )
 
-    def coarse_sends(src, dst, ssem, rsem, act):
+    def coarse_sends(src, dst, ssem, rsem, act, own):
         for idx, j in enumerate(coarse):
-
-            @pl.when(layer == j)
+            reach = [t for i, t in tops if i < idx or (own and i == idx)]
+            if reach:
+
+                @pl.when(layer == j)
+                def _():
+                    for n, t in enumerate(reach[::-1]):
+                        act(send(src, dst.at[idx], ssem.at[n], rsem.at[idx], layer=jnp.int32(t)))
+
+    def lazy_sends(act):
+        for i, t in tops:
+            low = coarse[i - 1] if i else 0
+
+            @pl.when(layer == t)
             def _():
-                for n, t in enumerate(targets(j)):
-                    act(send(src, dst.at[idx], ssem.at[n], rsem.at[idx], layer=jnp.int32(t)))
-
+                for n, target in enumerate(range(low, t)):
+                    act(send(err_bf, err_in, s_lz.at[n], r_lz.at[0], layer=jnp.int32(target)))
+
+    for load in small[1:3]:
+        load.wait()
     pl.when(layer > 0)(lambda: up_guess().start())
     start = lambda c: c.start()
-    coarse_sends(guess_ref, cguess, s_cg, r_cg, start)
-    coarse_sends(rate_ref, crate, s_cr, r_cr, start)
+    coarse_sends(rate_ref, crate, s_cr, r_cr, start, True)
+    coarse_sends(guess_ref, cguess, s_cg, r_cg, start, False)
+    for load in small[:1] + small[3:]:
+        load.wait()
 
     gain1, gain2 = gain1_ref[...], gain2_ref[...]
     loads[0].wait()
@@ -311,21 +334,25 @@
     relaxed[...] = backward(False)
     plain_sender = (layer > 0) & jnp.logical_not(is_coarse)
     pl.when(plain_sender)(lambda: up_relaxed().start())
-    coarse_sends(relaxed, crel, s_ce, r_ce, start)
+    coarse_sends(relaxed, crel, s_ce, r_ce, start, True)
 
     def build_err():
-        err[...] = jnp.zeros_like(err)
-        for idx in reversed(range(len(coarse))):
-
-            @pl.when(layer < coarse[idx])
+        here = jnp.int32(0)
+        for i, t in tops:
+
+            @pl.when(layer == t)
             def _():
-                here = jnp.int32(0)
-                send(guess_ref, cguess.at[idx], s_cg.at[0], r_cg.at[idx], layer=here).wait_recv()
-                send(rate_ref, crate.at[idx], s_cr.at[0], r_cr.at[idx], layer=here).wait_recv()
-                send(relaxed, crel.at[idx], s_ce.at[0], r_ce.at[idx], layer=here).wait_recv()
-                err[...] = crate[idx] * err[...] + (
-                    crel[idx].astype(F32) - cguess[idx].astype(F32)
-                )
+                for idx in reversed(range(i, len(coarse))):
+                    send(rate_ref, crate.at[idx], s_cr.at[0], r_cr.at[idx], layer=here).wait_recv()
+                    if idx > i:
+                        send(guess_ref, cguess.at[idx], s_cg.at[0], r_cg.at[idx], layer=here).wait_recv()
+                    send(relaxed, crel.at[idx], s_ce.at[0], r_ce.at[idx], layer=here).wait_recv()
+                    old = above[...] if idx == i else cguess[idx]
+                    resid = crel[idx].astype(F32) - old.astype(F32)
+                    above_it = idx < len(coarse) - 1
+                    err[...] = crate[idx] * err[...] + resid if above_it else resid
+
+        err_bf[...] = err[...].astype(BF)
 
     @pl.when(is_last)
     def _():
@@ -340,6 +367,7 @@
     def _():
         build_err()
         up_bf[...] = (above[...].astype(F32) + err[...]).astype(BF)
+        lazy_sends(start)
 
     adj_ref[...] = backward(True)
 
@@ -351,7 +379,15 @@
     for o in range(1, dpn):
         gain_send(o).start()
     to_chips(3)
-    pl.when(jnp.logical_not(next_coarse))(build_err)
+
+    @pl.when(is_last)
+    def _():
+        err[...] = jnp.zeros_like(err)
+
+    @pl.when(next_plain)
+    def _():
+        send(err_bf, err_in, s_lz.at[0], r_lz.at[0], layer=jnp.int32(0)).wait_recv()
+        err[...] = err_in[...].astype(F32)
 
     @pl.when(is_coarse)
     def _():
@@ -359,7 +395,7 @@
         err[...] = rate_ref[...] * err[...] + (relaxed[...].astype(F32) - own)
         adj_ref[...] = (own + err[...]).astype(BF)
 
-    err_out[...] = err[...]
+    err_ref[...] = err[...]
     finish(0)
     finish(1)
     gains = gsum[...]
@@ -381,9 +417,10 @@
     sent = lambda c: c.wait_send()
     pl.when(layer > 0)(lambda: sent(up_guess()))
     pl.when(plain_sender)(lambda: sent(up_relaxed()))
-    coarse_sends(guess_ref, cguess, s_cg, r_cg, sent)
-    coarse_sends(rate_ref, crate, s_cr, r_cr, sent)
-    coarse_sends(relaxed, crel, s_ce, r_ce, sent)
+    coarse_sends(guess_ref, cguess, s_cg, r_cg, sent, False)
+    coarse_sends(rate_ref, crate, s_cr, r_cr, sent, True)
+    coarse_sends(relaxed, crel, s_ce, r_ce, sent, True)
+    lazy_sends(sent)
     for g in range(4):
         for i in range(chips):
             sent(near(g, i))
@@ -391,6 +428,19 @@
             sent(far(g, o))
     for o in range(1, dpn):
         sent(gain_send(o))
+
+
+def writer(*refs):
+    n = len(refs) // 2
+    sems = refs[-1]
+    copies = [
+        pltpu.make_async_copy(refs[i], refs[n + i].at[0] if len(refs[n + i].shape) == 3 else refs[n + i], sems.at[i])
+        for i in range(n)
+    ]
+    for copy in copies:
+        copy.start()
+    for copy in copies:
+        copy.wait()
 
 
 def on_device(layers, dpn, *args):
@@ -405,7 +455,10 @@
     vm = pltpu.VMEM
     rows = (tokens, width)
     dma = lambda *s: pltpu.SemaphoreType.DMA(s)
+    line = vm((1, width), F32)
     scratch = [
+        vm(rows, BF), vm(rows, BF), vm(rows, BF),
+        line, line, line,
         vm((width, 3 * width), BF), vm((width, width), BF), vm((width, ff), BF),
         vm((ff, width), BF),
         vm((tokens, 3 * width), BF), vm((SEQ, SEQ), F32),
@@ -415,7 +468,7 @@
         vm(rows, BF), vm(rows, BF), vm((tokens, 3 * width), BF), vm((tokens, ff), BF),
         vm(rows, F32), vm(rows, BF),
         vm(rows, BF), vm(rows, BF), vm((n,) + rows, BF), vm((n,) + rows, BF),
-        vm((n, 1, width), F32), vm(rows, F32),
+        vm((n, 1, width), F32), vm(rows, F32), vm(rows, BF), vm(rows, BF),
     ]
     scratch += [vm(s, BF) for s in shapes]
     scratch += [vm((chips, s[0] // dpn, s[1]), BF) for s in shapes]
@@ -423,34 +476,46 @@
     scratch += [vm((2, width), F32), vm((dpn - 1, 2, width), F32)]
     far = max(chips - 1, 1)
     scratch += [
-        dma(4), dma(2), dma(2), dma(layers), dma(n), dma(layers), dma(n), dma(layers), dma(n),
+        dma(4), dma(6), dma(2), dma(2), dma(n), dma(n), dma(n), dma(n), dma(n), dma(n),
+        dma(FACTOR), dma(1),
         dma(4, chips), dma(4, chips), dma(4, far), dma(4, far), dma(dpn - 1), dma(dpn - 1),
     ]
+    left = pl.BlockSpec(memory_space=pltpu.HBM)
     whole = pl.BlockSpec(memory_space=pltpu.VMEM)
-    left = pl.BlockSpec(memory_space=pl.ANY)
-    out = lambda s, t: jax.ShapeDtypeStruct(s, t)
-    piece = lambda s: out((s[0] // dpn, s[1]), BF)
+    piece = lambda s: vm((s[0] // dpn, s[1]), F32)
+    small = vm((1, width // dpn), F32)
     results = pl.pallas_call(
         functools.partial(kernel, layers, dpn, coarse),
         out_shape=(
-            out(rows, BF), out(rows, F32), piece(shapes[3]), piece(shapes[2]), piece(shapes[1]),
-            piece(shapes[0]), out((1, width // dpn), F32), out((1, width // dpn), F32),
+            vm(rows, BF), vm(rows, F32), piece(shapes[3]), piece(shapes[2]), piece(shapes[1]),
+            piece(shapes[0]), small, small,
         ),
-        in_specs=[pl.BlockSpec(memory_space=pltpu.SMEM)] + [whole] * 6 + [left] * 4,
+        in_specs=[pl.BlockSpec(memory_space=pltpu.SMEM)] + [left] * 10,
         out_specs=(whole,) * 8,
         scratch_shapes=scratch,
         compiler_params=pltpu.CompilerParams(
-            collective_id=0, has_side_effects=True, vmem_limit_bytes=56 * 1024 * 1024
+            collective_id=0, has_side_effects=True, vmem_limit_bytes=48 * 1024 * 1024
         ),
     )(
-        lengths, states[0], guess[0], cotangent, rate, gain1, gain2,
-        w_qkv[0], w_out[0], w_in[0], w_back[0],
+        lengths,
+        *(
+            pltpu.with_memory_space_constraint(a, pltpu.HBM)
+            for a in (
+                states[0], guess[0], cotangent, rate, gain1, gain2,
+                w_qkv[0], w_out[0], w_in[0], w_back[0],
+            )
+        )
     )
-    adj, err, g_qkv, g_out, g_in, g_back, g_one, g_two = results
-    return (
-        adj[None], err[None], g_qkv.astype(F32)[None], g_out.astype(F32)[None],
-        g_in.astype(F32)[None], g_back.astype(F32)[None], g_one, g_two,
-    )
+    results = [pltpu.with_memory_space_constraint(r, pltpu.VMEM) for r in results]
+    shape = lambda r: r.shape if r.shape[0] == 1 else (1,) + r.shape
+    return pl.pallas_call(
+        writer,
+        out_shape=tuple(jax.ShapeDtypeStruct(shape(r), r.dtype) for r in results),
+        in_specs=[whole] * 8,
+        out_specs=(left,) * 8,
+        scratch_shapes=[dma(8)],
+        compiler_params=pltpu.CompilerParams(vmem_limit_bytes=1024 * 1024),
+    )(*results)
 
 
 def solution(mesh):

time: 98.1 us -> 71.4 us (0.73)
  the two profiles are of different devices: /device:TPU:15 before, /device:TPU:0 now
where the time goes in v1:
time: 71.4 us; the launch traced here: 71.3 us
  Pallas kernels  70 us (98%)
  between operations  1.29 us (2%)
    pallas_call x1, Pallas kernels, on_device(): pl.pallas_call(functools.partial(kernel, layers, dpn, coarse), out_shape=...  68 us
    pallas_call x1, Pallas kernels, on_device(): pl.pallas_call(writer, out_shape=tuple((jax.ShapeDtypeStruct(shape(r), r....  2 us

profile of v1, /device:TPU:0, one launch (start us, length us, event | category | flops | bytes accessed | tf_op | source)
XLA Modules:
  0.0 71.3 jit_solution(16518075391376421740)
XLA Ops:
  1.3 68.0 %shard_map.170 = (bf16[256,512]{1,0:T(8,128)(2,1)S(1)}, f32[256,512]{1,0:T(8,128)S(1)}, f32[128,1536]{1,0:T(8,128)S(1)}, f32[128,512]{1,0:T(8,128)S(1)}, f32[128...) custom-call(s32[1]{0:T(128)S(6)} %copy.19.len_ref, ...), custom_call_target="tpu_custom_call" | custom-call | tf_op jit(solution)/shard_map/pallas_call | solution.py:487
  69.3 2.0 %shard_map.171 = (bf16[1,256,512]{2,1,0:T(8,128)(2,1)}, f32[1,256,512]{2,1,0:T(8,128)}, f32[1,128,1536]{2,1,0:T(8,128)}, f32[1,128,512]{2,1,0:T(8,128)}, f32[1,1...) custom-call(bf16[256,512]{1,0:T(8,128)(2,1)S(1)} %get-tuple-element.16.refs_0_, ...), custom_call_target="tpu_custom_call" | custom-call | tf_op jit(solution)/shard_map/pallas_call | solution.py:511

commit v2 on v1

--- a/solution.py
+++ b/solution.py
@@ -60,8 +60,11 @@
     r1_back, r1_in, r1_out, r1_qkv,
     r2_back, r2_in, r2_out, r2_qkv,
     gsum, grecv,
+    x_far, ctx_far, normed_far, d2_far, d1_far, dpre_far, d2_bf, unit1_far, inv1_far,
+    hidden_far, deriv_far, x_t, half_s, half_r, quarter_s, quarter_r, small_s, small_r,
+    pq, pq1, pq2,
     wsem, lsem, s_up, r_up, s_cg, r_cg, s_cr, r_cr, s_ce, r_ce, s_lz, r_lz,
-    s1, q1, s2, q2, s_g, r_g,
+    s1, q1, s2, q2, s_g, r_g, s_mate, r_mate, s_half, r_half, sq1, rq1, sq2, rq2,
 ):
     layer = lax.axis_index("layer")
     dp = lax.axis_index("dp")
@@ -72,6 +75,8 @@
     scale = HEAD_DIM ** (-0.5)
     chips = dpn // 2
     chip, core = dp // 2, dp % 2
+    paired = chips == 2
+    mate, sibling = 2 * (1 - chip) + core, 2 * chip + 1 - core
     last = layers - 1
     is_last = layer == last
     is_coarse = (layer % FACTOR == 0) | is_last
@@ -150,7 +155,14 @@
     start = lambda c: c.start()
     coarse_sends(rate_ref, crate, s_cr, r_cr, start, True)
     coarse_sends(guess_ref, cguess, s_cg, r_cg, start, False)
-    for load in small[:1] + small[3:]:
+    small[0].wait()
+    to_mate = lambda i, src, dst: send(src, dst, s_mate.at[i], r_mate.at[i], dp=mate)
+    mate_x = lambda: to_mate(0, x_ref, x_far)
+    mate_ctx = lambda: to_mate(1, ctx, ctx_far)
+    mate_d2 = lambda: to_mate(2, d2_bf, d2_far)
+    if paired:
+        mate_x().start()
+    for load in small[3:]:
         load.wait()
 
     gain1, gain2 = gain1_ref[...], gain2_ref[...]
@@ -177,6 +189,8 @@
             return carry
 
         lax.fori_loop(0, pairs, attend, 0)
+    if paired:
+        mate_ctx().start()
     loads[1].wait()
     u, iv = unit_of(DEPTH_GAIN * x_ref[...].astype(F32) + nn(ctx[...], wout[...]))
     unit1[...] = u
@@ -185,18 +199,22 @@
     loads[2].wait()
     step = 512
 
-    def feed(i, carry):
-        lanes = pl.ds(pl.multiple_of(i * step, step), step)
-        pre = nn(normed_bf[...], win[:, lanes])
-        sq = pre * pre
-        t = jnp.tanh(TANH_SCALE * (pre + CUBIC * sq * pre))
-        hidden[:, lanes] = (0.5 * pre * (1.0 + t)).astype(BF)
-        deriv[:, lanes] = 0.5 * (1.0 + t) + 0.5 * pre * (1.0 - t * t) * TANH_SCALE * (
-            1.0 + 3.0 * CUBIC * sq
-        )
-        return carry
-
-    lax.fori_loop(0, hidden_units // step, feed, 0)
+    def feed_forward(normed, out, slope):
+        def feed(i, carry):
+            lanes = pl.ds(pl.multiple_of(i * step, step), step)
+            pre = nn(normed[...], win[:, lanes])
+            sq = pre * pre
+            t = jnp.tanh(TANH_SCALE * (pre + CUBIC * sq * pre))
+            out[:, lanes] = (0.5 * pre * (1.0 + t)).astype(BF)
+            slope[:, lanes] = 0.5 * (1.0 + t) + 0.5 * pre * (1.0 - t * t) * TANH_SCALE * (
+                1.0 + 3.0 * CUBIC * sq
+            )
+            return carry
+
+        with jax.named_scope("feed"):
+            lax.fori_loop(0, hidden_units // step, feed, 0)
+
+    feed_forward(normed_bf, hidden, deriv)
     loads[3].wait()
     u, iv = unit_of(DEPTH_GAIN * (unit1[...] * gain1) + nn(hidden[...], wback[...]))
     unit2[...] = u
@@ -261,6 +279,33 @@
 
         lax.fori_loop(0, left.shape[1] // cols, body, 0)
 
+    def hidden_back(d, slope, out):
+        def body(i, carry):
+            lanes = pl.ds(pl.multiple_of(i * step, step), step)
+            out[:, lanes] = (nt(d[...], wback[lanes, :]) * slope[:, lanes]).astype(BF)
+            return carry
+
+        with jax.named_scope("du"):
+            lax.fori_loop(0, hidden_units // step, body, 0)
+
+    def attend_back(s, i):
+        rows = pl.ds(s * SEQ, SEQ)
+        lanes = lambda k: pl.ds(pl.multiple_of(k * width + i * 128, 128), 128)
+        q, k, v = qkv[rows, lanes(0)], qkv[rows, lanes(1)], qkv[rows, lanes(2)]
+        dc = dctx[rows, lanes(0)]
+        outs = ([], [], [])
+        for h in range(2):
+            cut = slice(h * HEAD_DIM, (h + 1) * HEAD_DIM)
+            p = probs[s, 2 * i + h]
+            dp_ = nt(dc[:, cut], v[:, cut])
+            outs[2].append(tn(p.astype(BF), dc[:, cut]))
+            ds = p * (dp_ - jnp.sum(p * dp_, axis=-1, keepdims=True)) * scale
+            ds = ds.astype(BF)
+            outs[0].append(nn(ds, k[:, cut]))
+            outs[1].append(tn(ds, q[:, cut]))
+        for n in range(3):
+            dqkv[rows, lanes(n)] = jnp.concatenate(outs[n], axis=-1).astype(BF)
+
     def backward(final):
         up = up_bf[...].astype(F32)
         d2, grad_two = norm_back(up, unit2[...], inv2[...], gain2)
@@ -273,13 +318,7 @@
             transposed(hidden, up_bf[...], part_back)
             to_partner(0)
 
-        def body(i, carry):
-            lanes = pl.ds(pl.multiple_of(i * step, step), step)
-            dh = nt(up_bf[...], wback[lanes, :])
-            dpre[:, lanes] = (dh * deriv[:, lanes]).astype(BF)
-            return carry
-
-        lax.fori_loop(0, hidden_units // step, body, 0)
+        hidden_back(up_bf, deriv, dpre)
         if final:
             to_chips(0)
             transposed(normed_bf, dpre[...], part_in)
@@ -295,33 +334,119 @@
             to_partner(2)
         dctx[...] = nt(up_bf[...], wout[...]).astype(BF)
         for s in range(sentences):
-            rows = pl.ds(s * SEQ, SEQ)
 
             def attend(i, carry):
-                lanes = lambda k: pl.ds(pl.multiple_of(k * width + i * 128, 128), 128)
-                q, k, v = qkv[rows, lanes(0)], qkv[rows, lanes(1)], qkv[rows, lanes(2)]
-                dc = dctx[rows, lanes(0)]
-                outs = ([], [], [])
-                for h in range(2):
-                    cut = slice(h * HEAD_DIM, (h + 1) * HEAD_DIM)
-                    p = probs[s, 2 * i + h]
-                    dp_ = nt(dc[:, cut], v[:, cut])
-                    outs[2].append(tn(p.astype(BF), dc[:, cut]))
-                    ds = p * (dp_ - jnp.sum(p * dp_, axis=-1, keepdims=True)) * scale
-                    ds = ds.astype(BF)
-                    outs[0].append(nn(ds, k[:, cut]))
-                    outs[1].append(tn(ds, q[:, cut]))
-                for n in range(3):
-                    dqkv[rows, lanes(n)] = jnp.concatenate(outs[n], axis=-1).astype(BF)
+                attend_back(s, i)
                 return carry
 
-            lax.fori_loop(0, pairs, attend, 0)
+            with jax.named_scope("att2"):
+                lax.fori_loop(0, pairs, attend, 0)
         if final:
             to_chips(2)
             transposed(x_ref, dqkv[...], part_qkv)
             to_partner(3)
         return (dfirst[...] + nt(dqkv[...], wqkv[...])).astype(BF)
 
+    def half_send(g):
+        src, dst = ((half_s, half_r), (quarter_s, quarter_r), (small_s, small_r))[g]
+        return send(src, dst, s_half.at[g], r_half.at[g], dp=sibling)
+
+    def near_qkv(i, c):
+        size = pq.shape[1] // dpn
+        at = pl.multiple_of((2 * c + 1 - core) * size, size)
+        return send(
+            pq.at[i, pl.ds(at, size)], pq1.at[i, c], sq1.at[i, c], rq1.at[i, c], dp=sibling
+        )
+
+    def mine_qkv(i, c):
+        size = pq.shape[1] // dpn
+        at = pl.multiple_of((2 * c + core) * size, size)
+        return pq[i, pl.ds(at, size)].astype(F32)
+
+    def far_qkv(i):
+        return send(pq1.at[i, 1 - chip], pq2.at[i], sq2.at[i], rq2.at[i], dp=mate)
+
+    def relay_qkv(i):
+        near_qkv(i, 1 - chip).wait_recv()
+        pq1[i, 1 - chip] = (pq1[i, 1 - chip].astype(F32) + mine_qkv(i, 1 - chip)).astype(BF)
+        far_qkv(i).start()
+
+    def finish_qkv(i):
+        near_qkv(i, chip).wait_recv()
+        total = pq1[i, chip].astype(F32) + mine_qkv(i, chip)
+        far_qkv(i).wait_recv()
+        total = total + pq2[i].astype(F32)
+        for n in range(3):
+            gqkv_ref[:, n * width + i * 128 : n * width + (i + 1) * 128] = total[
+                :, n * 128 : (n + 1) * 128
+            ]
+
+    def rows_of(left, left_far, right, right_far, c, size):
+        at = pl.ds(pl.multiple_of((2 * chip + c) * size, size), size)
+        return tn(left[:, at], right[...]) + tn(left_far[:, at], right_far[...])
+
+    def look_ahead():
+        mate_x().wait_recv()
+        mate_ctx().wait_recv()
+        u, iv = unit_of(DEPTH_GAIN * x_far[...].astype(F32) + nn(ctx_far[...], wout[...]))
+        unit1_far[...] = u
+        inv1_far[...] = iv
+        normed_far[...] = (u * gain1).astype(BF)
+        feed_forward(normed_far, hidden_far, deriv_far)
+        x_t[...] = x_ref[...].T
+
+    def backward_paired():
+        d2, grad_two = norm_back(up_bf[...].astype(F32), unit2[...], inv2[...], gain2)
+        d2_bf[...] = d2.astype(BF)
+        mate_d2().start()
+        dfirst[...] = DEPTH_GAIN * d2
+        gsum[1:2, :] = grad_two
+        hidden_back(d2_bf, deriv, dpre)
+        d1, grad_one = norm_back(dfirst[...] + nt(dpre[...], win[...]), unit1[...], inv1[...], gain1)
+        dfirst[...] = DEPTH_GAIN * d1
+        up_bf[...] = d1.astype(BF)
+        gsum[0:1, :] = grad_one
+        for o in range(1, dpn):
+            gain_send(o).start()
+        dctx[...] = nt(up_bf[...], wout[...]).astype(BF)
+        for i in range(pairs):
+            with jax.named_scope("att2"):
+                for s in range(sentences):
+                    attend_back(s, i)
+            with jax.named_scope("gqkv"):
+                cut = [dqkv[:, n * width + i * 128 : n * width + (i + 1) * 128] for n in range(3)]
+                pq[i] = nn(x_t[...], jnp.concatenate(cut, axis=-1)).astype(BF)
+                near_qkv(i, 1 - chip).start()
+                near_qkv(i, chip).start()
+            if i:
+                relay_qkv(i - 1)
+        with jax.named_scope("wd2"):
+            mate_d2().wait_recv()
+        hidden_back(d2_far, deriv_far, dpre_far)
+        relay_qkv(pairs - 1)
+        d2o = d2_far[...].astype(F32)
+        d1, _ = norm_back(
+            DEPTH_GAIN * d2o + nt(dpre_far[...], win[...]), unit1_far[...], inv1_far[...], gain1
+        )
+        d1_far[...] = d1.astype(BF)
+        parts = (
+            (hidden, hidden_far, d2_bf, d2_far, half_s, gback_ref),
+            (normed_bf, normed_far, dpre, dpre_far, quarter_s, gin_ref),
+            (ctx, ctx_far, up_bf, d1_far, small_s, gout_ref),
+        )
+        with jax.named_scope("gpart"):
+            for g, (a, a_far, b, b_far, out, _) in enumerate(parts):
+                out[...] = rows_of(a, a_far, b, b_far, 1 - core, out.shape[0]).astype(BF)
+                half_send(g).start()
+            for a, a_far, b, b_far, _, out in parts:
+                out[...] = rows_of(a, a_far, b, b_far, core, out.shape[0])
+        return (dfirst[...] + nt(dqkv[...], wqkv[...])).astype(BF)
+
+    def gain_send(o):
+        return send(
+            gsum, grecv.at[o - 1], s_g.at[o - 1], r_g.at[o - 1], dp=lax.rem(dp + o, dpn)
+        )
+
     @pl.when(is_last)
     def _():
         up_bf[...] = cot_ref[...]
@@ -335,6 +460,8 @@
     plain_sender = (layer > 0) & jnp.logical_not(is_coarse)
     pl.when(plain_sender)(lambda: up_relaxed().start())
     coarse_sends(relaxed, crel, s_ce, r_ce, start, True)
+    if paired:
+        look_ahead()
 
     def build_err():
         here = jnp.int32(0)
@@ -369,16 +496,13 @@
         up_bf[...] = (above[...].astype(F32) + err[...]).astype(BF)
         lazy_sends(start)
 
-    adj_ref[...] = backward(True)
-
-    def gain_send(o):
-        return send(
-            gsum, grecv.at[o - 1], s_g.at[o - 1], r_g.at[o - 1], dp=lax.rem(dp + o, dpn)
-        )
-
-    for o in range(1, dpn):
-        gain_send(o).start()
-    to_chips(3)
+    if paired:
+        adj_ref[...] = backward_paired()
+    else:
+        adj_ref[...] = backward(True)
+        for o in range(1, dpn):
+            gain_send(o).start()
+        to_chips(3)
 
     @pl.when(is_last)
     def _():
@@ -396,8 +520,9 @@
         adj_ref[...] = (own + err[...]).astype(BF)
 
     err_ref[...] = err[...]
-    finish(0)
-    finish(1)
+    if not paired:
+        finish(0)
+        finish(1)
     gains = gsum[...]
     for o in range(1, dpn):
         gain_send(o).wait_recv()
@@ -411,8 +536,18 @@
         two = two + jnp.where(here, gains[1:2, cut], 0.0)
     g1_ref[...] = one
     g2_ref[...] = two
-    finish(2)
-    finish(3)
+    if paired:
+        for g, (part, out) in enumerate(
+            ((half_r, gback_ref), (quarter_r, gin_ref), (small_r, gout_ref))
+        ):
+            half_send(g).wait_recv()
+            out[...] = out[...] + part[...].astype(F32)
+        with jax.named_scope("finq"):
+            for i in range(pairs):
+                finish_qkv(i)
+    else:
+        finish(2)
+        finish(3)
 
     sent = lambda c: c.wait_send()
     pl.when(layer > 0)(lambda: sent(up_guess()))
@@ -421,11 +556,21 @@
     coarse_sends(rate_ref, crate, s_cr, r_cr, sent, True)
     coarse_sends(relaxed, crel, s_ce, r_ce, sent, True)
     lazy_sends(sent)
-    for g in range(4):
-        for i in range(chips):
-            sent(near(g, i))
-        for o in range(1, chips):
-            sent(far(g, o))
+    if paired:
+        for copy in (mate_x(), mate_ctx(), mate_d2()):
+            sent(copy)
+        for g in range(3):
+            sent(half_send(g))
+        for i in range(pairs):
+            sent(near_qkv(i, 0))
+            sent(near_qkv(i, 1))
+            sent(far_qkv(i))
+    else:
+        for g in range(4):
+            for i in range(chips):
+                sent(near(g, i))
+            for o in range(1, chips):
+                sent(far(g, o))
     for o in range(1, dpn):
         sent(gain_send(o))
 
@@ -470,15 +615,32 @@
         vm(rows, BF), vm(rows, BF), vm((n,) + rows, BF), vm((n,) + rows, BF),
         vm((n, 1, width), F32), vm(rows, F32), vm(rows, BF), vm(rows, BF),
     ]
-    scratch += [vm(s, BF) for s in shapes]
-    scratch += [vm((chips, s[0] // dpn, s[1]), BF) for s in shapes]
-    scratch += [vm((max(chips - 1, 1), s[0] // dpn, s[1]), BF) for s in shapes]
+    paired = chips == 2
+    pairs = width // 128
+    far = max(chips - 1, 1)
+    tile = (8, 128)
+    either = lambda use, s, t=BF: vm(s if use else tile, t)
+    scratch += [either(not paired, s) for s in shapes]
+    scratch += [either(not paired, (chips, s[0] // dpn, s[1])) for s in shapes]
+    scratch += [either(not paired, (far, s[0] // dpn, s[1])) for s in shapes]
     scratch += [vm((2, width), F32), vm((dpn - 1, 2, width), F32)]
-    far = max(chips - 1, 1)
+    scratch += [either(paired, rows) for _ in range(5)]
+    scratch += [
+        either(paired, (tokens, ff)), either(paired, rows), either(paired, rows, F32),
+        either(paired, (tokens, 1), F32), either(paired, (tokens, ff)),
+        either(paired, (tokens, ff), F32), either(paired, (width, tokens)),
+    ]
+    for s in (shapes[0], shapes[1], shapes[2]):
+        scratch += [either(paired, (s[0] // dpn, s[1])) for _ in range(2)]
+    scratch += [
+        either(paired, (pairs, width, 384)), either(paired, (pairs, 2, width // dpn, 384)),
+        either(paired, (pairs, width // dpn, 384)),
+    ]
     scratch += [
         dma(4), dma(6), dma(2), dma(2), dma(n), dma(n), dma(n), dma(n), dma(n), dma(n),
         dma(FACTOR), dma(1),
         dma(4, chips), dma(4, chips), dma(4, far), dma(4, far), dma(dpn - 1), dma(dpn - 1),
+        dma(3), dma(3), dma(3), dma(3), dma(pairs, 2), dma(pairs, 2), dma(pairs), dma(pairs),
     ]
     left = pl.BlockSpec(memory_space=pltpu.HBM)
     whole = pl.BlockSpec(memory_space=pltpu.VMEM)

time: 71.4 us -> 48.6 us (0.68)
  Pallas kernels: 70 us -> 47 us
    pallas_call x1, Pallas kernels: 68 us -> 45 us  [on_device(): pl.pallas_call(functools.partial(kernel, layers, dpn, coarse), out_shape=...]
where the time goes in v2:
time: 48.6 us; the launch traced here: 48.5 us
  Pallas kernels  47 us (97%)
  between operations  1.45 us (3%)
    pallas_call x1, Pallas kernels, on_device(): pl.pallas_call(functools.partial(kernel, layers, dpn, coarse), out_shape=...  45 us
    pallas_call x1, Pallas kernels, on_device(): pl.pallas_call(writer, out_shape=tuple((jax.ShapeDtypeStruct(shape(r), r....  2 us

profile of v2, /device:TPU:0, one launch (start us, length us, event | category | flops | bytes accessed | tf_op | source)
XLA Modules:
  0.0 48.5 jit_solution(17121108189758135310)
XLA Ops:
  1.3 45.0 %shard_map.170 = (bf16[256,512]{1,0:T(8,128)(2,1)S(1)}, f32[256,512]{1,0:T(8,128)S(1)}, f32[128,1536]{1,0:T(8,128)S(1)}, f32[128,512]{1,0:T(8,128)S(1)}, f32[128...) custom-call(s32[1]{0:T(128)S(6)} %copy.19.len_ref, ...), custom_call_target="tpu_custom_call" | custom-call | tf_op jit(solution)/shard_map/pallas_call | solution.py:649
  46.3 2.0 %shard_map.171 = (bf16[1,256,512]{2,1,0:T(8,128)(2,1)}, f32[1,256,512]{2,1,0:T(8,128)}, f32[1,128,1536]{2,1,0:T(8,128)}, f32[1,128,512]{2,1,0:T(8,128)}, f32[1,1...) custom-call(bf16[256,512]{1,0:T(8,128)(2,1)S(1)} %get-tuple-element.16.refs_0_, ...), custom_call_target="tpu_custom_call" | custom-call | tf_op jit(solution)/shard_map/pallas_call | solution.py:673

commit v3 on v2

--- a/solution.py
+++ b/solution.py
@@ -47,7 +47,7 @@
 
 
 def kernel(
-    layers, dpn, coarse,
+    layers, dpn, coarse, cuts,
     len_ref, x_hbm, guess_hbm, cot_hbm, rate_hbm, gain1_hbm, gain2_hbm,
     wqkv_hbm, wout_hbm, win_hbm, wback_hbm,
     adj_ref, err_ref, gqkv_ref, gout_ref, gin_ref, gback_ref, g1_ref, g2_ref,
@@ -62,7 +62,7 @@
     gsum, grecv,
     x_far, ctx_far, normed_far, d2_far, d1_far, dpre_far, d2_bf, unit1_far, inv1_far,
     hidden_far, deriv_far, x_t, half_s, half_r, quarter_s, quarter_r, small_s, small_r,
-    pq, pq1, pq2,
+    pq, pq1, pq2, q_t, dctx_t,
     wsem, lsem, s_up, r_up, s_cg, r_cg, s_cr, r_cr, s_ce, r_ce, s_lz, r_lz,
     s1, q1, s2, q2, s_g, r_g, s_mate, r_mate, s_half, r_half, sq1, rq1, sq2, rq2,
 ):
@@ -105,7 +105,7 @@
             )
         )
     ]
-    for load in small[:3] + loads[:1] + small[3:] + loads[1:]:
+    for load in small[:1] + loads[:1] + small[1:] + loads[1:]:
         load.start()
 
     barrier = pltpu.get_barrier_semaphore()
@@ -119,16 +119,33 @@
             barrier, inc=1, device_id={"dp": lax.rem(dp + o, dpn)},
             device_id_type=pl.DeviceIdType.MESH,
         )
-    pl.semaphore_wait(barrier, layers - 1 + dpn - 1)
-
     tops = [(i, c - 1) for i, c in enumerate(coarse)]
 
-    up_guess = lambda: send(
-        guess_ref, above, s_up.at[0], r_up.at[0], layer=jnp.maximum(layer - 1, 0)
-    )
-    up_relaxed = lambda: send(
-        relaxed, above2, s_up.at[1], r_up.at[1], layer=jnp.maximum(layer - 1, 0)
-    )
+    part_rows = tokens // cuts
+    span = lambda r: pl.ds(r * part_rows, part_rows)
+    down = jnp.maximum(layer - 1, 0)
+
+    def up_guess(r):
+        at = span(r)
+        return send(guess_ref.at[at], above.at[at], s_up.at[0, r], r_up.at[0, r], layer=down)
+
+    def up_relaxed(r):
+        at = span(r)
+        return send(relaxed.at[at], above2.at[at], s_up.at[1, r], r_up.at[1, r], layer=down)
+
+    def crel_send(idx, n, r, target):
+        at = span(r)
+        return send(
+            relaxed.at[at], crel.at[idx, at], s_ce.at[n, r], r_ce.at[idx, r], layer=target
+        )
+
+    def crel_sends(r, act):
+        for idx, j in enumerate(coarse):
+
+            @pl.when(layer == j)
+            def _():
+                for n in range(idx + 1):
+                    act(crel_send(idx, n, r, jnp.int32(coarse[idx - n] - 1)))
 
     def coarse_sends(src, dst, ssem, rsem, act, own):
         for idx, j in enumerate(coarse):
@@ -151,31 +168,33 @@
 
     for load in small[1:3]:
         load.wait()
-    pl.when(layer > 0)(lambda: up_guess().start())
+    pl.semaphore_wait(barrier, layers - 1 + dpn - 1)
     start = lambda c: c.start()
+
+    @pl.when(layer > 0)
+    def _():
+        for r in range(cuts):
+            up_guess(r).start()
+
     coarse_sends(rate_ref, crate, s_cr, r_cr, start, True)
-    coarse_sends(guess_ref, cguess, s_cg, r_cg, start, False)
     small[0].wait()
     to_mate = lambda i, src, dst: send(src, dst, s_mate.at[i], r_mate.at[i], dp=mate)
     mate_x = lambda: to_mate(0, x_ref, x_far)
     mate_ctx = lambda: to_mate(1, ctx, ctx_far)
-    mate_d2 = lambda: to_mate(2, d2_bf, d2_far)
+    mate_d2 = lambda r: to_mate(2 + r, d2_bf.at[span(r)], d2_far.at[span(r)])
     if paired:
         mate_x().start()
-    for load in small[3:]:
-        load.wait()
-
-    gain1, gain2 = gain1_ref[...], gain2_ref[...]
     loads[0].wait()
     qkv[...] = nn(x_ref[...], wqkv[...]).astype(BF)
+    q_t[...] = qkv[:, :width].T
     for s in range(sentences):
         rows = pl.ds(s * SEQ, SEQ)
         row_at = lax.broadcasted_iota(jnp.int32, (SEQ, SEQ), 0)
         col_at = lax.broadcasted_iota(jnp.int32, (SEQ, SEQ), 1)
         bias[...] = jnp.where((col_at <= row_at) & (col_at < len_ref[s]), 0.0, -1e30)
 
-        def attend(i, carry):
-            lanes = lambda k: pl.ds(pl.multiple_of(k * width + i * 128, 128), 128)
+        def attend(i):
+            lanes = lambda k: pl.ds(k * width + i * 128, 128)
             q, k, v = qkv[rows, lanes(0)], qkv[rows, lanes(1)], qkv[rows, lanes(2)]
             outs = []
             for h in range(2):
@@ -186,11 +205,15 @@
                 probs[s, 2 * i + h] = p
                 outs.append(nn(p.astype(BF), v[:, cut]))
             ctx[rows, lanes(0)] = jnp.concatenate(outs, axis=-1).astype(BF)
-            return carry
-
-        lax.fori_loop(0, pairs, attend, 0)
+
+        for i in range(pairs):
+            attend(i)
+    coarse_sends(guess_ref, cguess, s_cg, r_cg, start, False)
     if paired:
         mate_ctx().start()
+    for load in small[3:]:
+        load.wait()
+    gain1, gain2 = gain1_ref[...], gain2_ref[...]
     loads[1].wait()
     u, iv = unit_of(DEPTH_GAIN * x_ref[...].astype(F32) + nn(ctx[...], wout[...]))
     unit1[...] = u
@@ -200,8 +223,8 @@
     step = 512
 
     def feed_forward(normed, out, slope):
-        def feed(i, carry):
-            lanes = pl.ds(pl.multiple_of(i * step, step), step)
+        def feed(i):
+            lanes = pl.ds(i * step, step)
             pre = nn(normed[...], win[:, lanes])
             sq = pre * pre
             t = jnp.tanh(TANH_SCALE * (pre + CUBIC * sq * pre))
@@ -209,10 +232,10 @@
             slope[:, lanes] = 0.5 * (1.0 + t) + 0.5 * pre * (1.0 - t * t) * TANH_SCALE * (
                 1.0 + 3.0 * CUBIC * sq
             )
-            return carry
 
         with jax.named_scope("feed"):
-            lax.fori_loop(0, hidden_units // step, feed, 0)
+            for i in range(hidden_units // step):
+                feed(i)
 
     feed_forward(normed_bf, hidden, deriv)
     loads[3].wait()
@@ -280,72 +303,76 @@
         lax.fori_loop(0, left.shape[1] // cols, body, 0)
 
     def hidden_back(d, slope, out):
-        def body(i, carry):
-            lanes = pl.ds(pl.multiple_of(i * step, step), step)
-            out[:, lanes] = (nt(d[...], wback[lanes, :]) * slope[:, lanes]).astype(BF)
-            return carry
-
         with jax.named_scope("du"):
-            lax.fori_loop(0, hidden_units // step, body, 0)
-
-    def attend_back(s, i):
-        rows = pl.ds(s * SEQ, SEQ)
-        lanes = lambda k: pl.ds(pl.multiple_of(k * width + i * 128, 128), 128)
-        q, k, v = qkv[rows, lanes(0)], qkv[rows, lanes(1)], qkv[rows, lanes(2)]
-        dc = dctx[rows, lanes(0)]
-        outs = ([], [], [])
-        for h in range(2):
-            cut = slice(h * HEAD_DIM, (h + 1) * HEAD_DIM)
-            p = probs[s, 2 * i + h]
-            dp_ = nt(dc[:, cut], v[:, cut])
-            outs[2].append(tn(p.astype(BF), dc[:, cut]))
-            ds = p * (dp_ - jnp.sum(p * dp_, axis=-1, keepdims=True)) * scale
-            ds = ds.astype(BF)
-            outs[0].append(nn(ds, k[:, cut]))
-            outs[1].append(tn(ds, q[:, cut]))
-        for n in range(3):
-            dqkv[rows, lanes(n)] = jnp.concatenate(outs[n], axis=-1).astype(BF)
-
-    def backward(final):
-        up = up_bf[...].astype(F32)
-        d2, grad_two = norm_back(up, unit2[...], inv2[...], gain2)
-        d2_bf = d2.astype(BF)
-        dfirst[...] = DEPTH_GAIN * d2
-        up_bf[...] = d2_bf
-
+            for i in range(hidden_units // step):
+                lanes = pl.ds(i * step, step)
+                out[:, lanes] = (nt(d[...], wback[lanes, :]) * slope[:, lanes]).astype(BF)
+
+    def to_second(r, final):
+        at = span(r)
+        d2, grad_two = norm_back(up_bf[at, :].astype(F32), unit2[at, :], inv2[at, :], gain2)
+        d2_bf[at, :] = d2.astype(BF)
+        if final and paired:
+            mate_d2(r).start()
+        dfirst[at, :] = DEPTH_GAIN * d2
         if final:
-            gsum[1:2, :] = grad_two
-            transposed(hidden, up_bf[...], part_back)
-            to_partner(0)
-
-        hidden_back(up_bf, deriv, dpre)
-        if final:
-            to_chips(0)
-            transposed(normed_bf, dpre[...], part_in)
-            to_partner(1)
+            gsum[1:2, :] = grad_two if r == 0 else gsum[1:2, :] + grad_two
+
+    def to_scores(final):
+        hidden_back(d2_bf, deriv, dpre)
         dn = dfirst[...] + nt(dpre[...], win[...])
         d1, grad_one = norm_back(dn, unit1[...], inv1[...], gain1)
         dfirst[...] = DEPTH_GAIN * d1
         up_bf[...] = d1.astype(BF)
         if final:
             gsum[0:1, :] = grad_one
-            to_chips(1)
-            transposed(ctx, up_bf[...], part_out)
-            to_partner(2)
         dctx[...] = nt(up_bf[...], wout[...]).astype(BF)
-        for s in range(sentences):
-
-            def attend(i, carry):
-                attend_back(s, i)
-                return carry
-
-            with jax.named_scope("att2"):
-                lax.fori_loop(0, pairs, attend, 0)
-        if final:
-            to_chips(2)
-            transposed(x_ref, dqkv[...], part_qkv)
-            to_partner(3)
-        return (dfirst[...] + nt(dqkv[...], wqkv[...])).astype(BF)
+        dctx_t[...] = dctx[...].T
+
+    def to_state(out):
+        with jax.named_scope("dstate"):
+            out[...] = (dfirst[...] + nt(dqkv[...], wqkv[...])).astype(BF)
+
+    def attend_back(s, i):
+        rows = pl.ds(s * SEQ, SEQ)
+        lanes = lambda k: pl.ds(k * width + i * 128, 128)
+        k, v = qkv[rows, lanes(1)], qkv[rows, lanes(2)]
+        dc = dctx[rows, lanes(0)]
+        outs = ([], [], [])
+        for h in range(2):
+            cut = slice(h * HEAD_DIM, (h + 1) * HEAD_DIM)
+            own = pl.ds(i * 128 + h * HEAD_DIM, HEAD_DIM)
+            p = probs[s, 2 * i + h]
+            dp_ = nt(dc[:, cut], v[:, cut])
+            outs[2].append(nn(dctx_t[own, rows], p.astype(BF)))
+            ds = p * (dp_ - jnp.sum(p * dp_, axis=-1, keepdims=True)) * scale
+            ds = ds.astype(BF)
+            outs[0].append(nn(ds, k[:, cut]))
+            outs[1].append(nn(q_t[own, rows], ds))
+        dqkv[rows, lanes(0)] = jnp.concatenate(outs[0], axis=-1).astype(BF)
+        for n in (1, 2):
+            dqkv[rows, lanes(n)] = jnp.concatenate(outs[n], axis=0).astype(BF).T
+
+    def attention_back():
+        with jax.named_scope("att2"):
+            for s in range(sentences):
+                for i in range(pairs):
+                    attend_back(s, i)
+
+    def backward_summed():
+        transposed(hidden, d2_bf[...], part_back)
+        to_partner(0)
+        transposed(normed_bf, dpre[...], part_in)
+        to_partner(1)
+        to_chips(0)
+        transposed(ctx, up_bf[...], part_out)
+        to_partner(2)
+        to_chips(1)
+        attention_back()
+        to_chips(2)
+        transposed(x_ref, dqkv[...], part_qkv)
+        to_partner(3)
+        to_state(adj_ref)
 
     def half_send(g):
         src, dst = ((half_s, half_r), (quarter_s, quarter_r), (small_s, small_r))[g]
@@ -396,19 +423,6 @@
         x_t[...] = x_ref[...].T
 
     def backward_paired():
-        d2, grad_two = norm_back(up_bf[...].astype(F32), unit2[...], inv2[...], gain2)
-        d2_bf[...] = d2.astype(BF)
-        mate_d2().start()
-        dfirst[...] = DEPTH_GAIN * d2
-        gsum[1:2, :] = grad_two
-        hidden_back(d2_bf, deriv, dpre)
-        d1, grad_one = norm_back(dfirst[...] + nt(dpre[...], win[...]), unit1[...], inv1[...], gain1)
-        dfirst[...] = DEPTH_GAIN * d1
-        up_bf[...] = d1.astype(BF)
-        gsum[0:1, :] = grad_one
-        for o in range(1, dpn):
-            gain_send(o).start()
-        dctx[...] = nt(up_bf[...], wout[...]).astype(BF)
         for i in range(pairs):
             with jax.named_scope("att2"):
                 for s in range(sentences):
@@ -421,7 +435,8 @@
             if i:
                 relay_qkv(i - 1)
         with jax.named_scope("wd2"):
-            mate_d2().wait_recv()
+            for r in range(cuts):
+                mate_d2(r).wait_recv()
         hidden_back(d2_far, deriv_far, dpre_far)
         relay_qkv(pairs - 1)
         d2o = d2_far[...].astype(F32)
@@ -440,68 +455,94 @@
                 half_send(g).start()
             for a, a_far, b, b_far, _, out in parts:
                 out[...] = rows_of(a, a_far, b, b_far, core, out.shape[0])
-        return (dfirst[...] + nt(dqkv[...], wqkv[...])).astype(BF)
+        to_state(adj_ref)
 
     def gain_send(o):
         return send(
             gsum, grecv.at[o - 1], s_g.at[o - 1], r_g.at[o - 1], dp=lax.rem(dp + o, dpn)
         )
 
-    @pl.when(is_last)
-    def _():
-        up_bf[...] = cot_ref[...]
-
-    @pl.when(layer < last)
-    def _():
-        up_guess().wait_recv()
-        up_bf[...] = above[...]
-
-    relaxed[...] = backward(False)
+    for r in range(cuts):
+
+        @pl.when(is_last)
+        def _():
+            up_bf[span(r), :] = cot_ref[span(r), :]
+
+        @pl.when(layer < last)
+        def _():
+            up_guess(r).wait_recv()
+            up_bf[span(r), :] = above[span(r), :]
+
+        to_second(r, False)
+
+    to_scores(False)
+
+    attention_back()
     plain_sender = (layer > 0) & jnp.logical_not(is_coarse)
-    pl.when(plain_sender)(lambda: up_relaxed().start())
-    coarse_sends(relaxed, crel, s_ce, r_ce, start, True)
+    to_state(relaxed)
+    for r in range(cuts):
+
+        @pl.when(plain_sender)
+        def _():
+            up_relaxed(r).start()
+
+        crel_sends(r, start)
     if paired:
         look_ahead()
 
-    def build_err():
+    def build_err(r):
+        at = span(r)
         here = jnp.int32(0)
         for i, t in tops:
 
             @pl.when(layer == t)
             def _():
                 for idx in reversed(range(i, len(coarse))):
-                    send(rate_ref, crate.at[idx], s_cr.at[0], r_cr.at[idx], layer=here).wait_recv()
-                    if idx > i:
-                        send(guess_ref, cguess.at[idx], s_cg.at[0], r_cg.at[idx], layer=here).wait_recv()
-                    send(relaxed, crel.at[idx], s_ce.at[0], r_ce.at[idx], layer=here).wait_recv()
-                    old = above[...] if idx == i else cguess[idx]
-                    resid = crel[idx].astype(F32) - old.astype(F32)
+                    if r == 0:
+                        send(rate_ref, crate.at[idx], s_cr.at[0], r_cr.at[idx], layer=here).wait_recv()
+                        if idx > i:
+                            send(guess_ref, cguess.at[idx], s_cg.at[0], r_cg.at[idx], layer=here).wait_recv()
+                    crel_send(idx, 0, r, here).wait_recv()
+                    old = above[at, :] if idx == i else cguess[idx, at, :]
+                    resid = crel[idx, at, :].astype(F32) - old.astype(F32)
                     above_it = idx < len(coarse) - 1
-                    err[...] = crate[idx] * err[...] + resid if above_it else resid
-
-        err_bf[...] = err[...].astype(BF)
-
-    @pl.when(is_last)
-    def _():
-        up_bf[...] = cot_ref[...]
-
-    @pl.when(next_plain)
-    def _():
-        up_relaxed().wait_recv()
-        up_bf[...] = above2[...]
+                    err[at, :] = crate[idx] * err[at, :] + resid if above_it else resid
+
+        err_bf[at, :] = err[at, :].astype(BF)
+
+    for r in range(cuts):
+
+        @pl.when(is_last)
+        def _():
+            up_bf[span(r), :] = cot_ref[span(r), :]
+
+        @pl.when(next_plain)
+        def _():
+            with jax.named_scope("wrel"):
+                up_relaxed(r).wait_recv()
+            up_bf[span(r), :] = above2[span(r), :]
+
+        @pl.when(next_coarse)
+        def _():
+            with jax.named_scope("werr"):
+                build_err(r)
+            up_bf[span(r), :] = (above[span(r), :].astype(F32) + err[span(r), :]).astype(BF)
+
+        to_second(r, True)
+
+    to_scores(True)
+
+    for o in range(1, dpn):
+        gain_send(o).start()
 
     @pl.when(next_coarse)
     def _():
-        build_err()
-        up_bf[...] = (above[...].astype(F32) + err[...]).astype(BF)
         lazy_sends(start)
 
     if paired:
-        adj_ref[...] = backward_paired()
+        backward_paired()
     else:
-        adj_ref[...] = backward(True)
-        for o in range(1, dpn):
-            gain_send(o).start()
+        backward_summed()
         to_chips(3)
 
     @pl.when(is_last)
@@ -550,14 +591,24 @@
         finish(3)
 
     sent = lambda c: c.wait_send()
-    pl.when(layer > 0)(lambda: sent(up_guess()))
-    pl.when(plain_sender)(lambda: sent(up_relaxed()))
+
+    @pl.when(layer > 0)
+    def _():
+        for r in range(cuts):
+            sent(up_guess(r))
+
+    @pl.when(plain_sender)
+    def _():
+        for r in range(cuts):
+            sent(up_relaxed(r))
+
+    for r in range(cuts):
+        crel_sends(r, sent)
     coarse_sends(guess_ref, cguess, s_cg, r_cg, sent, False)
     coarse_sends(rate_ref, crate, s_cr, r_cr, sent, True)
-    coarse_sends(relaxed, crel, s_ce, r_ce, sent, True)
     lazy_sends(sent)
     if paired:
-        for copy in (mate_x(), mate_ctx(), mate_d2()):
+        for copy in [mate_x(), mate_ctx()] + [mate_d2(r) for r in range(cuts)]:
             sent(copy)
         for g in range(3):
             sent(half_send(g))
@@ -596,6 +647,7 @@
     coarse = [j for j in range(1, layers) if j % FACTOR == 0 or j == layers - 1]
     n = len(coarse)
     chips = dpn // 2
+    cuts = 2 if tokens % 256 == 0 else 1
     shapes = ((ff, width), (width, ff), (width, width), (width, 3 * width))
     vm = pltpu.VMEM
     rows = (tokens, width)
@@ -626,7 +678,7 @@
     scratch += [vm((2, width), F32), vm((dpn - 1, 2, width), F32)]
     scratch += [either(paired, rows) for _ in range(5)]
     scratch += [
-        either(paired, (tokens, ff)), either(paired, rows), either(paired, rows, F32),
+        either(paired, (tokens, ff)), vm(rows, BF), either(paired, rows, F32),
         either(paired, (tokens, 1), F32), either(paired, (tokens, ff)),
         either(paired, (tokens, ff), F32), either(paired, (width, tokens)),
     ]
@@ -634,20 +686,21 @@
         scratch += [either(paired, (s[0] // dpn, s[1])) for _ in range(2)]
     scratch += [
         either(paired, (pairs, width, 384)), either(paired, (pairs, 2, width // dpn, 384)),
-        either(paired, (pairs, width // dpn, 384)),
+        either(paired, (pairs, width // dpn, 384)), vm((width, tokens), BF), vm((width, tokens), BF),
     ]
     scratch += [
-        dma(4), dma(6), dma(2), dma(2), dma(n), dma(n), dma(n), dma(n), dma(n), dma(n),
+        dma(4), dma(6), dma(2, cuts), dma(2, cuts), dma(n), dma(n), dma(n), dma(n),
+        dma(n, cuts), dma(n, cuts),
         dma(FACTOR), dma(1),
         dma(4, chips), dma(4, chips), dma(4, far), dma(4, far), dma(dpn - 1), dma(dpn - 1),
-        dma(3), dma(3), dma(3), dma(3), dma(pairs, 2), dma(pairs, 2), dma(pairs), dma(pairs),
+        dma(2 + cuts), dma(2 + cuts), dma(3), dma(3), dma(pairs, 2), dma(pairs, 2), dma(pairs), dma(pairs),
     ]
     left = pl.BlockSpec(memory_space=pltpu.HBM)
     whole = pl.BlockSpec(memory_space=pltpu.VMEM)
     piece = lambda s: vm((s[0] // dpn, s[1]), F32)
     small = vm((1, width // dpn), F32)
     results = pl.pallas_call(
-        functools.partial(kernel, layers, dpn, coarse),
+        functools.partial(kernel, layers, dpn, coarse, cuts),
         out_shape=(
             vm(rows, BF), vm(rows, F32), piece(shapes[3]), piece(shapes[2]), piece(shapes[1]),
             piece(shapes[0]), small, small,

time: 48.6 us -> 44 us (0.905)
  Pallas kernels: 47 us -> 42.4 us
    pallas_call x1, Pallas kernels: 45 us -> 40.4 us  [on_device(): pl.pallas_call(functools.partial(kernel, layers, dpn, coarse, cuts), out_...]
where the time goes in v3:
time: 44 us; the launch traced here: 43.9 us
  Pallas kernels  42.4 us (96%)
  between operations  1.45 us (3%)
    pallas_call x1, Pallas kernels, on_device(): pl.pallas_call(functools.partial(kernel, layers, dpn, coarse, cuts), out_...  40.4 us
    pallas_call x1, Pallas kernels, on_device(): pl.pallas_call(writer, out_shape=tuple((jax.ShapeDtypeStruct(shape(r), r....  2 us

profile of v3, /device:TPU:0, one launch (start us, length us, event | category | flops | bytes accessed | tf_op | source)
XLA Modules:
  0.0 43.9 jit_solution(11358146867608774107)
XLA Ops:
  1.3 40.4 %shard_map.170 = (bf16[256,512]{1,0:T(8,128)(2,1)S(1)}, f32[256,512]{1,0:T(8,128)S(1)}, f32[128,1536]{1,0:T(8,128)S(1)}, f32[128,512]{1,0:T(8,128)S(1)}, f32[128...) custom-call(s32[1]{0:T(128)S(6)} %copy.19.len_ref, ...), custom_call_target="tpu_custom_call" | custom-call | tf_op jit(solution)/shard_map/pallas_call | solution.py:702
  41.7 2.0 %shard_map.171 = (bf16[1,256,512]{2,1,0:T(8,128)(2,1)}, f32[1,256,512]{2,1,0:T(8,128)}, f32[1,128,1536]{2,1,0:T(8,128)}, f32[1,128,512]{2,1,0:T(8,128)}, f32[1,1...) custom-call(bf16[256,512]{1,0:T(8,128)(2,1)S(1)} %get-tuple-element.16.refs_0_, ...), custom_call_target="tpu_custom_call" | custom-call | tf_op jit(solution)/shard_map/pallas_call | solution.py:726
